TPU v7x, 32 devices: a whole 2x2x4 slice. The times are simulated.
32 devices in a mesh: fsdp: 4 (over y, x), width: 8 (over z, core).
Axes of the slice: x: 2, y: 2, z: 4, core: 2. Of those that a mesh axis runs over, the one named last changes fastest.
Arguments:
- train_gate: float32 [4096, 11008], P('fsdp', 'width'), may hold values from -0.125 to 0.125
- drift_gate: float32 [4096, 11008], P('fsdp', 'width'), may hold values from -0.09375 to 0.09375
- spread_gate: float32 [4096, 11008], P('fsdp', 'width'), may hold values from -0.09375 to 0.09375
- train_up: float32 [4096, 11008], P('fsdp', 'width'), may hold values from -0.125 to 0.125
- drift_up: float32 [4096, 11008], P('fsdp', 'width'), may hold values from -0.09375 to 0.09375
- spread_up: float32 [4096, 11008], P('fsdp', 'width'), may hold values from -0.09375 to 0.09375
- norm_train: float32 [4096], P(('fsdp', 'width')), may hold values from 0.25 to 1.75
- norm_step: float32 [4096], P(('fsdp', 'width')), may hold values from -0.3 to 0.3
Outputs:
- serving_gate: bfloat16 [4096, 11008], P(None, 'width')
- serving_up: bfloat16 [4096, 11008], P(None, 'width')
- scale_gate: float32 [11008], P('width')
- scale_up: float32 [11008], P('width')
- serve_norm: bfloat16 [4096], replicated
- whole_gate: float32 [4096, 11008], P('fsdp', 'width')
- whole_up: float32 [4096, 11008], P('fsdp', 'width')
All inputs are finite; a program needn't handle non-finite values.
Results may differ from a plain program's by a relative error of at most 0.0004.
Values may be sent and summed in bfloat16 or wider, within the bound.
A program may use at most 128 MiB of HBM per device.

v0:
```python
import jax
import jax.numpy as jnp
from jax import lax
from jax.sharding import PartitionSpec as P

learn_rate = 0.3
hold_rate = 0.9


def shards(
    train_gate, drift_gate, spread_gate, train_up, drift_up, spread_up, norm_train, norm_step
):
    hold_gate = hold_rate * drift_gate + spread_gate
    whole_gate = train_gate - learn_rate * hold_gate
    hold_up = hold_rate * drift_up + spread_up
    whole_up = train_up - learn_rate * hold_up
    total_gate, total_up = lax.psum(
        (jnp.sum(whole_gate * whole_gate, axis=0), jnp.sum(whole_up * whole_up, axis=0)), "fsdp"
    )
    scale_gate = jnp.sqrt(total_gate)
    scale_up = jnp.sqrt(total_up)
    narrow_gate, narrow_up = (
        (whole_gate / scale_gate).astype(jnp.bfloat16),
        (whole_up / scale_up).astype(jnp.bfloat16),
    )
    serving_gate, serving_up = (
        lax.all_gather(narrow_gate, "fsdp", axis=0, tiled=True),
        lax.all_gather(narrow_up, "fsdp", axis=0, tiled=True),
    )
    serve_norm = lax.all_gather(
        (norm_train + norm_step).astype(jnp.bfloat16), ("fsdp", "width"), axis=0, tiled=True
    )
    return (serving_gate, serving_up, scale_gate, scale_up, serve_norm, whole_gate, whole_up)


def solution(mesh):
    in_specs = (
        P("fsdp", "width"),
        P("fsdp", "width"),
        P("fsdp", "width"),
        P("fsdp", "width"),
        P("fsdp", "width"),
        P("fsdp", "width"),
        P(("fsdp", "width")),
        P(("fsdp", "width")),
    )
    out_specs = (
        P(None, "width"),
        P(None, "width"),
        P("width"),
        P("width"),
        P(),
        P("fsdp", "width"),
        P("fsdp", "width"),
    )
    return jax.shard_map(shards, mesh=mesh, in_specs=in_specs, out_specs=out_specs, check_vma=False)
```

profile of v0, /device:TPU:0, one launch (start us, length us, event | category | flops | bytes accessed | tf_op | source)
XLA Modules:
  0.0 294.1 jit_solution(4612063814202278182)
XLA Ops:
  7.2 0.0 all-gather.6.cloned.1.call-start
  7.2 16.3 %multiply_reduce_fusion = (f32[1376]{0:T(1024)S(1)}, f32[1024,1376]{0,1:T(8,128)}, f32[1376]{0:T(1024)S(1)}, f32[1024,1376]{0,1:T(8,128)}) fusion(f32[1024,1376]{0,1:T(8,128)} %param.11, f32[1024,1376]{0,1:T(8,128)} %param.13, f32[1024,1376]{0,1:T(8,128)} %param.12, f32[1024,1376]{0,1:T(8,128)} %param.8, f32[1024,1376]{0,1:T(8,128)} %param.10, ...), kind=kLoop, calls=%fused_computation.1 | loop fusion | flops 16905536 | bytes 45099776 | tf_op jit(solution)/shard_map/reduce_sum | solution.py:18
  23.5 17.5 %all-reduce = (f32[1376]{0:T(1024)S(1)}, f32[1376]{0:T(1024)S(1)}) all-reduce(f32[1376]{0:T(1024)S(1)} %get-tuple-element.13, f32[1376]{0:T(1024)S(1)} %get-tuple-element.9), channel_id=1, replica_groups=mesh['fsdp'=4,'width'=8] {'fsdp'}, use_global_device_ids=true, to_apply=%region_1.0 | all-reduce | flops 2752 | bytes 22016 | tf_op jit(solution)/shard_map/psum | solution.py:17
  41.1 0.0 copy-start
  41.1 4.9 %divide_convert_fusion = bf16[1024,1376]{0,1:T(8,128)(2,1)} fusion(f32[1024,1376]{0,1:T(8,128)} %get-tuple-element.28, f32[1376]{0:T(1024)S(1)} %sqrt.7), kind=kLoop, calls=%fused_computation | loop fusion | flops 2818048 | bytes 8459648 | tf_op jit(solution)/shard_map/convert_element_type | solution.py:24
  45.9 0.0 all-gather.6.cloned.1.call-update
  46.0 0.0 copy-done
  46.0 0.0 all-gather.4.cloned.1.call-start
  46.0 0.0 copy-start.1
  46.0 0.0 copy-start.2
  46.1 0.0 copy-start.3
  46.1 4.9 %divide_convert_fusion.1 = bf16[1024,1376]{0,1:T(8,128)(2,1)} fusion(f32[1024,1376]{0,1:T(8,128)} %get-tuple-element.27, f32[1376]{0:T(1024)S(1)} %sqrt.6), kind=kLoop, calls=%fused_computation.3 | loop fusion | flops 2818048 | bytes 8459648 | tf_op jit(solution)/shard_map/convert_element_type | solution.py:23
  50.9 0.0 all-gather.4.cloned.1.call-update
  51.0 0.0 copy-done.1
  51.0 0.0 copy-done.2
  51.0 0.0 copy-done.3
  51.0 39.2 %all-gather = bf16[32,1,128]{2,1,0:T(2,128)(2,1)S(1)} all-gather(bf16[1,1,128]{2,1,0:T(2,128)(2,1)S(1)} %convert_bitcast_fusion), channel_id=1, replica_groups=mesh['fsdp'=4,'width'=8] {'fsdp','width'}, dimensions={0}, use_global_device_ids=true | all-gather | bytes 8448 | tf_op jit(solution)/shard_map/all_gather | solution.py:30
  90.2 0.6 reduce
  90.8 66.2 %all-gather.6.cloned.1.call-done = bf16[4096,1376]{0,1:T(8,128)(2,1)} async-done(((bf16[1024,1376]{0,1:T(8,128)(2,1)}), bf16[4096,1376]{0,1:T(8,128)(2,1)}) %all-gather.6.cloned.1.call-update) | async-done | bytes 11272208 | tf_op jit(solution)/shard_map/all_gather | solution.py:28
  157.0 113.9 %all-gather.4.cloned.1.call-done = bf16[4096,1376]{0,1:T(8,128)(2,1)} async-done(((bf16[1024,1376]{0,1:T(8,128)(2,1)}), bf16[4096,1376]{0,1:T(8,128)(2,1)}) %all-gather.4.cloned.1.call-update) | async-done | bytes 11272208 | tf_op jit(solution)/shard_map/all_gather | solution.py:27
  270.9 0.0 slice-start
  270.9 0.0 slice-start.1
  270.9 0.0 slice-start.2
  271.0 11.9 %copy.17 = bf16[4096,1376]{0,1:T(8,128)(2,1)} copy(bf16[4096,1376]{0,1:T(8,128)(2,1)} %all-gather.4.cloned.1.call-done) | data formatting | bytes 22544384
  282.9 0.0 slice-done
  282.9 0.0 slice-done.1
  282.9 0.0 slice-done.2
  282.9 4.3 %copy.18 = bf16[4096,1376]{0,1:T(8,128)(2,1)} copy(bf16[4096,1376]{0,1:T(8,128)(2,1)S(1)} %bitcast.4) | data formatting | bytes 22544384
  (4 shorter events, 0.0 us)
Async XLA Ops:
  7.2 149.9 %all-gather.6.cloned.1.call-start = ((), (), s32[]{:S(2)}) async-start(), calls=%async_computation.1 | async-start | bytes 14090240 | tf_op jit(solution)/shard_map/all_gather | solution.py:28
  41.1 4.9 %copy-start = (f32[1376]{0:T(1024)}, f32[1376]{0:T(1024)S(1)}, u32[]{:S(2)}) copy-start(f32[1376]{0:T(1024)S(1)} %sqrt.7) | copy-start | bytes 16516
  46.0 225.0 %all-gather.4.cloned.1.call-start = ((), (), s32[]{:S(2)}) async-start(), calls=%async_computation | async-start | bytes 14090240 | tf_op jit(solution)/shard_map/all_gather | solution.py:27
  46.0 4.9 %copy-start.1 = (f32[1376]{0:T(1024)}, f32[1376]{0:T(1024)S(1)}, u32[]{:S(2)}) copy-start(f32[1376]{0:T(1024)S(1)} %sqrt.6) | copy-start | bytes 16516
  46.0 4.9 %copy-start.2 = (f32[128]{0:T(128)S(1)}, f32[128]{0:T(128)}, u32[]{:S(2)}) copy-start(f32[128]{0:T(128)} %param.14) | copy-start | bytes 1540
  46.1 4.9 %copy-start.3 = (f32[128]{0:T(128)S(1)}, f32[128]{0:T(128)}, u32[]{:S(2)}) copy-start(f32[128]{0:T(128)} %param.15) | copy-start | bytes 1540
  270.9 11.9 %slice-start = ((s8[11272192]{0:T(1024)(128)(4,1)}), s8[4194304]{0:T(1024)(128)(4,1)S(1)}, s32[]{:S(2)}) async-start(s8[11272192]{0:T(1024)(128)(4,1)} %bitcast.3), calls=%async_computation.2 | async-start | bytes 8388608
  270.9 11.9 %slice-start.1 = ((s8[11272192]{0:T(1024)(128)(4,1)}), s8[4194304]{0:T(1024)(128)(4,1)S(1)}, s32[]{:S(2)}) async-start(s8[11272192]{0:T(1024)(128)(4,1)} %bitcast.3), calls=%async_computation.3 | async-start | bytes 8388608
  270.9 11.9 %slice-start.2 = ((s8[11272192]{0:T(1024)(128)(4,1)}), s8[2883584]{0:T(1024)(128)(4,1)S(1)}, s32[]{:S(2)}) async-start(s8[11272192]{0:T(1024)(128)(4,1)} %bitcast.3), calls=%async_computation.4 | async-start | bytes 5767168
Sparse Core Ops, SparseCore 0:
  46.1 110.8 all-gather.5
  159.4 111.4 all-gather.3
where the time goes:
time: 294 us
  waiting for transfers between devices  180 us (61%)
  blocking collectives  56.7 us (19%)
  other arithmetic  26.7 us (9%)
  local copies, waits for them, and re-layouts  16.3 us (6%)
  between operations  14.1 us (5%)
    all_gather x1, waiting for transfers between devices, shards(): lax.all_gather(narrow_gate, 'fsdp', axis=0, tiled=True)  114 us
    all_gather x1, waiting for transfers between devices, shards(): lax.all_gather(narrow_up, 'fsdp', axis=0, tiled=True)  66.2 us
    all_gather x1, blocking collectives, shards(): lax.all_gather((norm_train + norm_step).astype(jnp.bfloat16), ('fsdp', 'w...  39.2 us
    psum x1, blocking collectives, shards(): lax.psum((jnp.sum(whole_gate * whole_gate, axis=0), jnp.sum(whole_up * wh...  17.5 us
    reduce_sum x1, other arithmetic, shards(): jnp.sum(whole_up * whole_up, axis=0)  16.3 us
    unnamed x16, local copies, waits for them, and re-layouts  16.3 us
  transfers between devices with their start and end apart: 2, of which 2 were waited for; matrix products, arithmetic and copies ran while one was open for 2% of the time, Pallas kernels for 0%

commit v1 on v0

v1 whole, which is shorter than its diff:
```python
import functools

import jax
import jax.numpy as jnp
from jax import lax
from jax.experimental import pallas as pl
from jax.experimental.pallas import tpu as pltpu
from jax.sharding import PartitionSpec as P

learn_rate = 0.3
hold_rate = 0.9
LANES = 128
SUB = 16
MESH = pl.DeviceIdType.MESH


def ring_order(n):
    side = int(round(n**0.5))
    if side * side != n or side % 2:
        return list(range(n))
    walk = [y * side for y in range(side)]
    for y in reversed(range(side)):
        columns = range(1, side) if (side - 1 - y) % 2 == 0 else reversed(range(1, side))
        walk += [y * side + x for x in columns]
    return walk


def pick(table, index):
    value = jnp.int32(table[0])
    for k in range(1, len(table)):
        value = jnp.where(index == k, jnp.int32(table[k]), value)
    return value


def groups_of(columns):
    first = min(2 * LANES, columns // 2 // LANES * LANES)
    return [(0, 0, first), (0, first, columns - first), (1, 0, columns)]


def gather_kernel(n, w, order, names, *refs):
    (tg, dg, sg, tu, du, su, nt, ns) = refs[:8]
    (out_g, out_u, whole_g, whole_u, scale_out, norm_out) = refs[8:14]
    (tv, dv, sv, nv, sums, q, norm_buf) = refs[14:21]
    (in_sem, put_sem, sum_send, sum_recv, ring_send, ring_recv, nf_send, nf_recv, nw_send, nw_recv) = refs[21:]
    f_axis, w_axis = names
    columns, rows = tg.shape
    groups = groups_of(columns)
    args = ((tg, dg, sg), (tu, du, su))
    outs, wholes = (out_g, out_u), (whole_g, whole_u)
    me = lax.axis_index(f_axis)
    mw = lax.axis_index(w_axis)
    half_ring = n // 2
    at = {d: i for i, d in enumerate(order)}
    right = pick([order[(at[d] + 1) % n] for d in range(n)], me)
    left = pick([order[(at[d] - 1) % n] for d in range(n)], me)

    loads = []
    for g, (m, c0, cn) in enumerate(groups):
        for k, buf in enumerate((tv, dv, sv)):
            copy = pltpu.make_async_copy(
                args[m][k].at[pl.ds(c0, cn)], buf.at[m, pl.ds(c0, cn)], in_sem.at[g, k]
            )
            copy.start()
            loads.append(copy)

    barrier = pltpu.get_barrier_semaphore()
    for k in range(1, n):
        pl.semaphore_signal(
            barrier, inc=1, device_id={f_axis: lax.rem(me + k, n)}, device_id_type=MESH
        )
    for k in range(1, w):
        pl.semaphore_signal(
            barrier, inc=1, device_id={w_axis: lax.rem(mw + k, w)}, device_id_type=MESH
        )

    norm_buf[me, mw] = nt[0] + ns[0]
    q[...] = jnp.zeros_like(q)

    def blocks(c0, cn, body):
        full = cn // LANES

        @pl.loop(0, full)
        def _(b):
            body(pl.multiple_of(c0 + b * LANES, LANES), LANES)

        if cn % LANES:
            body(c0 + full * LANES, cn % LANES)

    def step_block(m, c, cn):
        for r in range(0, cn, SUB):
            at_rows = pl.ds(c + r, SUB)
            part = None
            for l in range(0, rows, LANES):
                lanes = pl.ds(l, LANES)
                hold = hold_rate * dv[m, at_rows, lanes] + sv[m, at_rows, lanes]
                new = tv[m, at_rows, lanes] - learn_rate * hold
                tv[m, at_rows, lanes] = new
                part = new * new if part is None else part + new * new
            q[pl.ds(r, SUB), :] = part
        sums[m, me, :, pl.ds(c, LANES)] = jnp.sum(q[...].T, axis=0, keepdims=True)

    def narrow_block(m, c, cn):
        lanes = pl.ds(c, LANES)
        total = sums[m, 0, :, lanes]
        for k in range(1, n):
            total = total + sums[m, k, :, lanes]
        scale = jnp.sqrt(total)
        scale_out[m, :, lanes] = scale
        q[...] = jnp.broadcast_to(scale, (LANES, LANES)).T
        for r in range(0, cn, SUB):
            at_rows = pl.ds(c + r, SUB)
            by = q[pl.ds(r, SUB), :]
            for l in range(0, rows, LANES):
                lanes = pl.ds(l, LANES)
                nv[m, at_rows, lanes] = (tv[m, at_rows, lanes] / by).astype(jnp.bfloat16)

    puts = []
    sends = []

    def exchange(g):
        m, c0, cn = groups[g]
        lanes = pl.ds(c0, -(-cn // LANES) * LANES)
        for k in range(1, n):
            copy = pltpu.make_async_remote_copy(
                src_ref=sums.at[m, me, :, lanes],
                dst_ref=sums.at[m, me, :, lanes],
                send_sem=sum_send.at[g, k],
                recv_sem=sum_recv.at[g, k],
                device_id={f_axis: lax.rem(me + k, n)},
                device_id_type=MESH,
            )
            copy.start()
            sends.append(copy)

    def exchanged(g):
        m, c0, cn = groups[g]
        lanes = pl.ds(c0, -(-cn // LANES) * LANES)
        for k in range(1, n):
            come = lax.rem(me - k + n, n)
            pltpu.make_async_remote_copy(
                src_ref=sums.at[m, come, :, lanes],
                dst_ref=sums.at[m, come, :, lanes],
                send_sem=sum_send.at[g, k],
                recv_sem=sum_recv.at[g, k],
                device_id={f_axis: come},
                device_id_type=MESH,
            ).wait_recv()

    def ring_part(g, s, way):
        _, c0, cn = groups[g]
        if s < half_ring - 1:
            return c0, cn
        cut = cn // (2 * SUB) * SUB
        return (c0, cut) if way == 0 else (c0 + cut, cn - cut)

    def origin(s, way):
        shift = -s if way == 0 else s
        return pick([order[(at[d] + shift) % n] for d in range(n)], me)

    def ring_copy(g, s, way, sent):
        m = groups[g][0]
        c0, cn = ring_part(g, s, way)
        block = origin(s if sent else s + 1, way)
        place = outs[m].at[pl.ds(c0, cn), pl.ds(pl.multiple_of(block * rows, LANES), rows)]
        source = nv.at[m, pl.ds(c0, cn)] if s == 0 and sent else place
        return pltpu.make_async_remote_copy(
            src_ref=source,
            dst_ref=place,
            send_sem=ring_send.at[g, s, way],
            recv_sem=ring_recv.at[g, s, way],
            device_id={f_axis: right if way == 0 else left},
            device_id_type=MESH,
        )

    def ring_start(g, s):
        for way in (0, 1):
            copy = ring_copy(g, s, way, True)
            copy.start()
            sends.append(copy)

    def norm_copy(axis, index, k, size, send, recv, place):
        return pltpu.make_async_remote_copy(
            src_ref=place,
            dst_ref=place,
            send_sem=send.at[k],
            recv_sem=recv.at[k],
            device_id={axis: lax.rem(index + k, size)},
            device_id_type=MESH,
        )

    for g, (m, c0, cn) in enumerate(groups):
        for copy in loads[3 * g : 3 * g + 3]:
            copy.wait()
        blocks(c0, cn, functools.partial(step_block, m))
        if g == 0:
            pl.semaphore_wait(barrier, n - 1 + w - 1)
        exchange(g)
        put = pltpu.make_async_copy(
            tv.at[m, pl.ds(c0, cn)], wholes[m].at[pl.ds(c0, cn)], put_sem.at[g, 0]
        )
        put.start()
        puts.append(put)
        if g == 0:
            for k in range(1, n):
                copy = norm_copy(f_axis, me, k, n, nf_send, nf_recv, norm_buf.at[me, mw])
                copy.start()
                sends.append(copy)
        exchanged(g)
        blocks(c0, cn, functools.partial(narrow_block, m))
        ring_start(g, 0)
        put = pltpu.make_async_copy(
            nv.at[m, pl.ds(c0, cn)],
            outs[m].at[pl.ds(c0, cn), pl.ds(pl.multiple_of(me * rows, LANES), rows)],
            put_sem.at[g, 1],
        )
        put.start()
        puts.append(put)

    for k in range(1, n):
        come = lax.rem(me - k + n, n)
        norm_copy(f_axis, me, k, n, nf_send, nf_recv, norm_buf.at[come, mw]).wait_recv()
    for k in range(1, w):
        copy = norm_copy(w_axis, mw, k, w, nw_send, nw_recv, norm_buf.at[:, mw])
        copy.start()
        sends.append(copy)
    for k in range(1, w):
        come = lax.rem(mw - k + w, w)
        norm_copy(w_axis, mw, k, w, nw_send, nw_recv, norm_buf.at[:, come]).wait_recv()
    norm_out[...] = norm_buf[...]

    for s in range(half_ring):
        for g in range(len(groups)):
            for way in (0, 1):
                ring_copy(g, s, way, False).wait_recv()
            if s + 1 < half_ring:
                ring_start(g, s + 1)
    for copy in sends:
        copy.wait_send()
    for copy in puts:
        copy.wait()


def solution(mesh):
    names = mesh.axis_names
    n, w = mesh.shape["fsdp"], mesh.shape["width"]
    order = ring_order(n)

    def shards(tg, dg, sg, tu, du, su, nt, ns):
        rows, columns = tg.shape
        padded = -(-columns // LANES) * LANES
        length = nt.shape[0]
        wide = -(-length // LANES) * LANES

        def line(x):
            return jnp.pad(x, (0, wide - length)).reshape(1, 1, wide)

        groups = len(groups_of(columns))
        hbm = pl.BlockSpec(memory_space=pl.ANY)
        vmem = pl.BlockSpec(memory_space=pltpu.VMEM)
        dma = pltpu.SemaphoreType.DMA
        sent = 3 * 2 * columns * rows * 2
        out_g, out_u, whole_g, whole_u, scales, norm = pl.pallas_call(
            functools.partial(gather_kernel, n, w, order, names),
            out_shape=(
                jax.ShapeDtypeStruct((columns, n * rows), jnp.bfloat16),
                jax.ShapeDtypeStruct((columns, n * rows), jnp.bfloat16),
                jax.ShapeDtypeStruct((columns, rows), jnp.float32),
                jax.ShapeDtypeStruct((columns, rows), jnp.float32),
                jax.ShapeDtypeStruct((2, 1, padded), jnp.float32),
                jax.ShapeDtypeStruct((n, w, 1, wide), jnp.float32),
            ),
            in_specs=[hbm] * 6 + [vmem] * 2,
            out_specs=[hbm] * 4 + [vmem] * 2,
            scratch_shapes=[
                pltpu.VMEM((2, columns, rows), jnp.float32),
                pltpu.VMEM((2, columns, rows), jnp.float32),
                pltpu.VMEM((2, columns, rows), jnp.float32),
                pltpu.VMEM((2, columns, rows), jnp.bfloat16),
                pltpu.VMEM((2, n, 1, padded), jnp.float32),
                pltpu.VMEM((LANES, LANES), jnp.float32),
                pltpu.VMEM((n, w, 1, wide), jnp.float32),
                dma((groups, 3)),
                dma((groups, 2)),
                dma((groups, n)),
                dma((groups, n)),
                dma((groups, n // 2, 2)),
                dma((groups, n // 2, 2)),
                dma((n,)),
                dma((n,)),
                dma((w,)),
                dma((w,)),
            ],
            compiler_params=pltpu.CompilerParams(
                collective_id=0, has_side_effects=True, vmem_limit_bytes=60 * 1024 * 1024
            ),
            cost_estimate=pl.CostEstimate(
                flops=20 * columns * rows, bytes_accessed=16 * sent, transcendentals=0
            ),
        )(tg.T, dg.T, sg.T, tu.T, du.T, su.T, line(nt), line(ns))
        serve_norm = norm[..., :length].reshape(n * w * length).astype(jnp.bfloat16)
        return (
            out_g.T,
            out_u.T,
            scales[0, 0, :columns],
            scales[1, 0, :columns],
            serve_norm,
            whole_g.T,
            whole_u.T,
        )

    split = P("fsdp", "width")
    flat = P(("fsdp", "width"))
    return jax.shard_map(
        shards,
        mesh=mesh,
        in_specs=(split,) * 6 + (flat,) * 2,
        out_specs=(P(None, "width"), P(None, "width"), P("width"), P("width"), P(), split, split),
        check_vma=False,
    )
```

time: 294 us -> 225 us (0.77)
  Pallas kernels: 0 us -> 198 us
  waiting for transfers between devices: 180 us -> 0 us
  blocking collectives: 56.7 us -> 0 us
  other arithmetic: 26.7 us -> 1.36 us
  between operations: 14.1 us -> 0.68 us
  local copies, waits for them, and re-layouts: 16.3 us -> 25.1 us
    pallas_call x0 -> x1, Pallas kernels: none -> 198 us  [shards(): pl.pallas_call(functools.partial(gather_kernel, n, w, order, names), out_...]
    all_gather x2 -> x0, waiting for transfers between devices: 180 us -> none  [the longest x1 114 us: shards(): lax.all_gather(narrow_gate, 'fsdp', axis=0, tiled=True)]
    all_gather x1 -> x0, blocking collectives: 39.2 us -> none  [shards(): lax.all_gather((norm_train + norm_step).astype(jnp.bfloat16), ('fsdp', 'w...]
    psum x1 -> x0, blocking collectives: 17.5 us -> none  [shards(): lax.psum((jnp.sum(whole_gate * whole_gate, axis=0), jnp.sum(whole_up * wh...]
    reduce_sum x1 -> x0, other arithmetic: 16.3 us -> none  [shards(): jnp.sum(whole_up * whole_up, axis=0)]
    convert_element_type x2 -> x1, other arithmetic: 9.71 us -> 1.36 us  [shards(): serve_norm = norm[..., :length].reshape(n * w * length).astype(jnp.bfloat16)]
    unnamed x16 -> x18, local copies, waits for them, and re-layouts: 16.3 us -> 23.7 us
  transfers between devices with their start and end apart: 2 -> 0, of which waited for: 2 -> 0; matrix products, arithmetic and copies ran while one was open for 2% -> 0% of each run, Pallas kernels for 0% -> 0%
where the time goes in v1:
time: 225 us
  Pallas kernels  198 us (88%)
  local copies, waits for them, and re-layouts  25.1 us (11%)
    pallas_call x1, Pallas kernels, shards(): pl.pallas_call(functools.partial(gather_kernel, n, w, order, names), out_...  198 us
    unnamed x18, local copies, waits for them, and re-layouts  23.7 us

profile of v1, /device:TPU:0, one launch (start us, length us, event | category | flops | bytes accessed | tf_op | source)
XLA Modules:
  0.0 224.7 jit_solution(2258165634775288665)
XLA Ops:
  0.6 197.6 %shard_map.135 = (bf16[1376,4096]{1,0:T(8,128)(2,1)}, bf16[1376,4096]{1,0:T(8,128)(2,1)}, f32[1376,1024]{1,0:T(8,128)}, f32[1376,1024]{1,0:T(8,128)}, f32[2,1,1408]{2,1,0:T(1,128)}, /*index=5*/f32[4,8,1,128]{3,2,1,0:T(1,128)}) custom-call(f32[1376,1024]{1,0:T(8,128)} %bitcast.17, f32[1376,1024]{1,0:T(8,128)} %bitcast.18, f32[1376,1024]{1,0:T(8,128)} %bitcast.19, ...), custom_call_target="tpu_custom_call" | custom-call | flops 28180480 | bytes 270532608 | tf_op jit(solution)/shard_map/pallas_call | solution.py:262
  198.2 1.4 convert_reduce_fusion
  199.6 1.3 slice_reduce_fusion
  200.9 0.0 slice-start
  200.9 0.0 slice-start.1
  200.9 0.0 slice-start.2
  200.9 0.0 slice-start.5
  200.9 0.0 slice-start.3
  201.0 11.7 %copy.19 = bf16[4096,1376]{0,1:T(8,128)(2,1)} copy(bf16[4096,1376]{0,1:T(8,128)(2,1)} %bitcast.16) | data formatting | bytes 22544384
  212.7 0.0 slice-done
  212.7 0.0 slice-done.1
  212.7 0.0 slice-done.2
  212.7 0.0 slice-start.6
  212.7 0.0 slice-start.4
  212.7 5.7 %copy.20 = bf16[4096,1376]{0,1:T(8,128)(2,1)} copy(bf16[4096,1376]{0,1:T(8,128)(2,1)S(1)} %bitcast.15) | data formatting | bytes 22544384
  218.4 0.0 slice-done.5
  218.4 1.3 slice-done.6
  219.7 2.5 %copy.21 = f32[1024,1376]{0,1:T(8,128)} copy(f32[1024,1376]{0,1:T(8,128)S(1)} %bitcast.28) | data formatting | bytes 11272192
  222.2 0.0 slice-done.3
  222.2 0.0 slice-done.4
  222.2 2.5 %copy.22 = f32[1024,1376]{0,1:T(8,128)} copy(f32[1024,1376]{0,1:T(8,128)S(1)} %bitcast.25) | data formatting | bytes 11272192
  (3 shorter events, 0.0 us)
Async XLA Ops:
  200.9 11.7 %slice-start = ((s8[11272192]{0:T(1024)(128)(4,1)}), s8[4194304]{0:T(1024)(128)(4,1)S(1)}, s32[]{:S(2)}) async-start(s8[11272192]{0:T(1024)(128)(4,1)} %bitcast.13), calls=%async_computation | async-start | bytes 8388608
  200.9 11.7 %slice-start.1 = ((s8[11272192]{0:T(1024)(128)(4,1)}), s8[4194304]{0:T(1024)(128)(4,1)S(1)}, s32[]{:S(2)}) async-start(s8[11272192]{0:T(1024)(128)(4,1)} %bitcast.13), calls=%async_computation.1 | async-start | bytes 8388608
  200.9 11.7 %slice-start.2 = ((s8[11272192]{0:T(1024)(128)(4,1)}), s8[2883584]{0:T(1024)(128)(4,1)S(1)}, s32[]{:S(2)}) async-start(s8[11272192]{0:T(1024)(128)(4,1)} %bitcast.13), calls=%async_computation.2 | async-start | bytes 5767168
  200.9 17.5 %slice-start.5 = ((s8[5636096]{0:T(1024)(128)(4,1)}), s8[4194304]{0:T(1024)(128)(4,1)S(1)}, s32[]{:S(2)}) async-start(s8[5636096]{0:T(1024)(128)(4,1)} %bitcast.26), calls=%async_computation.5 | async-start | bytes 8388608
  200.9 21.3 %slice-start.3 = ((s8[5636096]{0:T(1024)(128)(4,1)}), s8[4194304]{0:T(1024)(128)(4,1)S(1)}, s32[]{:S(2)}) async-start(s8[5636096]{0:T(1024)(128)(4,1)} %bitcast.23), calls=%async_computation.3 | async-start | bytes 8388608
  212.7 7.0 %slice-start.6 = ((s8[5636096]{0:T(1024)(128)(4,1)}), s8[1441792]{0:T(1024)(128)(4,1)S(1)}, s32[]{:S(2)}) async-start(s8[5636096]{0:T(1024)(128)(4,1)} %bitcast.26), calls=%async_computation.6 | async-start | bytes 2883584
  212.7 9.5 %slice-start.4 = ((s8[5636096]{0:T(1024)(128)(4,1)}), s8[1441792]{0:T(1024)(128)(4,1)S(1)}, s32[]{:S(2)}) async-start(s8[5636096]{0:T(1024)(128)(4,1)} %bitcast.23), calls=%async_computation.4 | async-start | bytes 2883584
